TPU v7x, 32 devices: a whole 2x2x4 slice. The times are simulated.
32 devices in a mesh: gx: 8 (over y, x, core), gy: 4 (over z).
Axes of the slice: x: 2, y: 2, z: 4, core: 2. Of those that a mesh axis runs over, the one named last changes fastest.
Arguments:
- cost: float32 [16, 1024, 512], P(None, 'gx', 'gy'), may hold values from 0 to 7.5
- density_start: float32 [16, 1024, 512], P(None, 'gx', 'gy'), may hold values from 0.125 to 4.5
- coupling: float32 [16, 16], replicated, may hold values from 0 to 0.25
Outputs:
- value: float32 [16, 1024, 512], P(None, 'gx', 'gy')
- density: float32 [16, 1024, 512], P(None, 'gx', 'gy')
- ergodic: float32 [16], replicated
All inputs are finite; a program needn't handle non-finite values.
Results may differ from a plain program's by a relative error of at most 0.0003.
Values sent between devices are 32-bit elements; how exact they have to be, the bound alone decides.
A program may use at most 64 MiB of HBM per device.

v0:
```python
import jax
import jax.numpy as jnp
from jax import lax
from jax.sharding import PartitionSpec as P

SWEEPS = 5


viscosity = 0.5
theta = 2.0


def padded_2(cells, sides, width):
    for axis, dim in sides:
        count = lax.axis_size(axis)
        head = lax.slice_in_dim(cells, 0, width, axis=dim)
        tail = lax.slice_in_dim(cells, cells.shape[dim] - width, cells.shape[dim], axis=dim)
        cells = jnp.concatenate(
            [
                lax.ppermute(tail, axis, [(i, (i + 1) % count) for i in range(count)]),
                cells,
                lax.ppermute(head, axis, [((i + 1) % count, i) for i in range(count)]),
            ],
            axis=dim,
        )
    return cells


def rates(padded):
    u_xp = padded[:, 2:, 1:-1]
    u_xm = padded[:, :-2, 1:-1]
    u_yp = padded[:, 1:-1, 2:]
    u_ym = padded[:, 1:-1, :-2]
    vx = -(u_xp - u_xm) * 0.5
    vy = -(u_yp - u_ym) * 0.5
    r_xp = viscosity + jnp.maximum(vx, 0.0)
    r_xm = viscosity + jnp.maximum(-vx, 0.0)
    r_yp = viscosity + jnp.maximum(vy, 0.0)
    r_ym = viscosity + jnp.maximum(-vy, 0.0)
    total = r_xp + r_xm + r_yp + r_ym
    speed = (vx * vx + vy * vy) * 0.5
    return ((r_xp, r_xm, r_yp, r_ym), (u_xp, u_xm, u_yp, u_ym), total, speed)


def hjb_trial(padded, source, ergodic):
    (r_xp, r_xm, r_yp, r_ym), (u_xp, u_xm, u_yp, u_ym), total, speed = rates(padded)
    return (
        source
        + speed
        - ergodic[:, None, None]
        + r_xp * u_xp
        + r_xm * u_xm
        + r_yp * u_yp
        + r_ym * u_ym
    ) / total


def trial_shift(trial, cells):
    return lax.psum(jnp.sum(trial, axis=(1, 2)), ("gx", "gy")) / cells


def hjb_step(padded, source, ergodic, cells):
    trial = hjb_trial(padded, source, ergodic)
    shift = trial_shift(trial, cells)
    return (trial - shift[:, None, None], ergodic + theta * shift)


def inflow_weights(padded):
    (r_xp, r_xm, r_yp, r_ym), unused, total, speed = rates(padded)
    inner = total[:, 1:-1, 1:-1]
    return (
        r_xm[:, 2:, 1:-1] / inner,
        r_xp[:, :-2, 1:-1] / inner,
        r_ym[:, 1:-1, 2:] / inner,
        r_yp[:, 1:-1, :-2] / inner,
    )


def fp_step(padded, weights):
    c_xp, c_xm, c_yp, c_ym = weights
    return (
        c_xp * padded[:, 2:, 1:-1]
        + c_xm * padded[:, :-2, 1:-1]
        + c_yp * padded[:, 1:-1, 2:]
        + c_ym * padded[:, 1:-1, :-2]
    )


def class_mass(density, cells):
    return lax.psum(jnp.sum(density, axis=(1, 2)), ("gx", "gy")) / cells


def normalize(density, cells):
    return density / class_mass(density, cells)[:, None, None]


def shards(cost, density_start, coupling):
    cells = float(cost.shape[1] * lax.axis_size("gx") * cost.shape[2] * lax.axis_size("gy"))
    value = jnp.zeros(cost.shape, jnp.float32)
    density = density_start
    ergodic = jnp.zeros((cost.shape[0],), jnp.float32)
    source = cost + jnp.einsum("kj,jxy->kxy", coupling, density, precision=lax.Precision.HIGHEST)
    for sweep in range(SWEEPS):
        padded = padded_2(value, (("gx", 1), ("gy", 2)), 1)
        value, ergodic = hjb_step(padded, source, ergodic, cells)
    padded = padded_2(value, (("gx", 1), ("gy", 2)), 2)
    weights = inflow_weights(padded)
    for sweep in range(SWEEPS):
        beside_all = padded_2(density, (("gx", 1), ("gy", 2)), 1)
        density = fp_step(beside_all, weights)
    density = normalize(density, cells)
    return (value, density, ergodic)


def solution(mesh):
    placed = (P(None, "gx", "gy"), P(None, "gx", "gy"), P())
    return jax.shard_map(
        shards,
        mesh=mesh,
        in_specs=placed,
        out_specs=(P(None, "gx", "gy"), P(None, "gx", "gy"), P()),
        check_vma=False,
    )
```

profile of v0, /device:TPU:0, one launch (start us, length us, event | category | flops | bytes accessed | tf_op | source)
XLA Modules:
  0.0 486.7 jit_solution(8878178904643323792)
XLA Ops:
  1.2 2.9 collective-permute-start
  6.7 4.3 collective-permute-start.2
  14.1 3.1 collective-permute-done.3
  18.9 6.1 %fusion.48 = (f32[16]{0:T(128)S(1)}, f32[16,128,128]{2,0,1:T(8,128)}, f32[16,128,128]{2,0,1:T(8,128)S(1)}) fusion(f32[16,128,128]{2,0,1:T(8,128)S(1)} %broadcast.46, f32[16,1,128]{2,0,1:T(8,128)S(1)} %collective-permute-done, f32[16,1,128]{2,0,1:T(8,128)S(1)} %collective-permute-done.1, f32[16,130,1]{2,0,1:T(8,128)} %copy.20, f32[16,130,1]{2,0,1:T(8,128)} %copy.18, ...), kind=kOutput, calls=%fused_computation.178 | convolution fusion | flops 61079536 | bytes 5276992 | tf_op jit(solution)/shard_map/kj,jxy->kxy/dot_general | solution.py:102
  25.0 36.9 %psum.42 = f32[16]{0:T(128)S(1)} all-reduce(f32[16]{0:T(128)S(1)} %get-tuple-element.24), channel_id=1, replica_groups=mesh['gx'=8,'gy'=4] {'gx','gy'}, use_global_device_ids=true, to_apply=%region_1.0 | all-reduce | flops 16 | bytes 128 | tf_op jit(solution)/shard_map/psum | solution.py:59
  76.1 3.1 collective-permute-done.7
  80.9 3.6 fusion.47
  84.5 37.9 %psum.43 = f32[16]{0:T(128)S(1)} all-reduce(f32[16]{0:T(128)S(1)} %get-tuple-element.22), channel_id=1, replica_groups=mesh['gx'=8,'gy'=4] {'gx','gy'}, use_global_device_ids=true, to_apply=%region_3.0 | all-reduce | flops 16 | bytes 128 | tf_op jit(solution)/shard_map/psum | solution.py:59
  131.1 14.5 %collective-permute-start.10 = (f32[16,130,1]{1,0,2:T(8,128)S(1)}, f32[16,130,1]{1,0,2:T(8,128)S(1)}, u32[]{:S(2)}, u32[]{:S(2)}) collective-permute-start(f32[16,130,1]{1,0,2:T(8,128)S(1)} %copy.25), channel_id=1, source_target_pairs={{1,0},{2,1},{3,2},{0,3},{5,4},{6,5},{7,6},{4,7},{9,8},{10,9},{11,1... | collective-permute-start | bytes 24968 | tf_op jit(solution)/shard_map/ppermute | solution.py:22
  148.5 3.4 collective-permute-done.11
  153.6 3.6 fusion.46
  157.2 37.7 %psum.44 = f32[16]{0:T(128)S(1)} all-reduce(f32[16]{0:T(128)S(1)} %get-tuple-element.20), channel_id=1, replica_groups=mesh['gx'=8,'gy'=4] {'gx','gy'}, use_global_device_ids=true, to_apply=%region_5.0 | all-reduce | flops 16 | bytes 128 | tf_op jit(solution)/shard_map/psum | solution.py:59
  205.9 2.9 collective-permute-start.15
  215.0 3.6 fusion.45
  218.6 39.8 %psum.45 = f32[16]{0:T(128)S(1)} all-reduce(f32[16]{0:T(128)S(1)} %get-tuple-element.18), channel_id=1, replica_groups=mesh['gx'=8,'gy'=4] {'gx','gy'}, use_global_device_ids=true, to_apply=%region_7.0 | all-reduce | flops 16 | bytes 128 | tf_op jit(solution)/shard_map/psum | solution.py:59
  270.6 2.7 collective-permute-start.18
  278.5 3.8 fusion.44
  282.3 39.4 %psum.46 = f32[16]{0:T(128)S(1)} all-reduce(f32[16]{0:T(128)S(1)} %get-tuple-element.16), channel_id=1, replica_groups=mesh['gx'=8,'gy'=4] {'gx','gy'}, use_global_device_ids=true, to_apply=%region_9.0 | all-reduce | flops 16 | bytes 128 | tf_op jit(solution)/shard_map/psum | solution.py:59
  353.7 3.9 fusion.34
  374.9 4.7 fusion.27
  396.6 4.7 fusion.20
  418.2 4.7 fusion.13
  439.8 5.3 %fusion.42 = (f32[16]{0:T(128)S(1)}, f32[16,128,128]{2,0,1:T(8,128)}) fusion(f32[16,128,128]{2,0,1:T(8,128)} %get-tuple-element.15, f32[16,1,128]{2,0,1:T(8,128)S(1)} %collective-permute-done.40, f32[16,128,128]{2,0,1:T(8,128)} %copy-done.6, f32[16,1,128]{2,0,1:T(8,128)S(1)} %collective-permute-done.41, f32[16,130,1]{2,0,1:T(8,128)} %copy.67, ...), kind=kLoop, calls=%fused_computation.173 | loop fusion | flops 4194288 | bytes 6324544 | tf_op jit(solution)/shard_map/reduce_sum | solution.py:90
  445.1 38.7 %psum.47 = f32[16]{0:T(128)S(1)} all-reduce(f32[16]{0:T(128)S(1)} %get-tuple-element.9), channel_id=1, replica_groups=mesh['gx'=8,'gy'=4] {'gx','gy'}, use_global_device_ids=true, to_apply=%region_11.0 | all-reduce | flops 16 | bytes 128 | tf_op jit(solution)/shard_map/psum | solution.py:90
  (208 shorter events, 174.1 us)
Async XLA Ops:
  0.7 4.8 collective-permute-start.1
  1.2 4.3 collective-permute-start
  6.7 5.8 %collective-permute-start.2 = (f32[16,130,1]{1,0,2:T(8,128)S(1)}, f32[16,130,1]{1,0,2:T(8,128)S(1)}, u32[]{:S(2)}, u32[]{:S(2)}) collective-permute-start(f32[16,130,1]{1,0,2:T(8,128)S(1)} %copy.17), channel_id=1, source_target_pairs={{1,0},{2,1},{3,2},{0,3},{5,4},{6,5},{7,6},{4,7},{9,8},{10,9},{11,1... | collective-permute-start | bytes 24968 | tf_op jit(solution)/shard_map/ppermute | solution.py:22
  11.6 5.6 %collective-permute-start.3 = (f32[16,130,1]{1,0,2:T(8,128)S(1)}, f32[16,130,1]{1,0,2:T(8,128)S(1)}, u32[]{:S(2)}, u32[]{:S(2)}) collective-permute-start(f32[16,130,1]{1,0,2:T(8,128)S(1)} %copy.19), channel_id=1, source_target_pairs={{0,1},{1,2},{2,3},{3,0},{4,5},{5,6},{6,7},{7,4},{8,9},{9,10},{10,1... | collective-permute-start | bytes 24968 | tf_op jit(solution)/shard_map/ppermute | solution.py:20
  70.7 4.6 collective-permute-start.6
  73.6 5.6 %collective-permute-start.7 = (f32[16,130,1]{1,0,2:T(8,128)S(1)}, f32[16,130,1]{1,0,2:T(8,128)S(1)}, u32[]{:S(2)}, u32[]{:S(2)}) collective-permute-start(f32[16,130,1]{1,0,2:T(8,128)S(1)} %copy.23), channel_id=1, source_target_pairs={{0,1},{1,2},{2,3},{3,0},{4,5},{5,6},{6,7},{7,4},{8,9},{9,10},{10,1... | collective-permute-start | bytes 24968 | tf_op jit(solution)/shard_map/ppermute | solution.py:20
  131.1 16.6 %collective-permute-start.10 = (f32[16,130,1]{1,0,2:T(8,128)S(1)}, f32[16,130,1]{1,0,2:T(8,128)S(1)}, u32[]{:S(2)}, u32[]{:S(2)}) collective-permute-start(f32[16,130,1]{1,0,2:T(8,128)S(1)} %copy.25), channel_id=1, source_target_pairs={{1,0},{2,1},{3,2},{0,3},{5,4},{6,5},{7,6},{4,7},{9,8},{10,9},{11,1... | collective-permute-start | bytes 24968 | tf_op jit(solution)/shard_map/ppermute | solution.py:22
  146.3 5.6 %collective-permute-start.11 = (f32[16,130,1]{1,0,2:T(8,128)S(1)}, f32[16,130,1]{1,0,2:T(8,128)S(1)}, u32[]{:S(2)}, u32[]{:S(2)}) collective-permute-start(f32[16,130,1]{1,0,2:T(8,128)S(1)} %copy.27), channel_id=1, source_target_pairs={{0,1},{1,2},{2,3},{3,0},{4,5},{5,6},{6,7},{7,4},{8,9},{9,10},{10,1... | collective-permute-start | bytes 24968 | tf_op jit(solution)/shard_map/ppermute | solution.py:20
  205.9 7.4 %collective-permute-start.15 = (f32[16,130,1]{1,0,2:T(8,128)S(1)}, f32[16,130,1]{1,0,2:T(8,128)S(1)}, u32[]{:S(2)}, u32[]{:S(2)}) collective-permute-start(f32[16,130,1]{1,0,2:T(8,128)S(1)} %copy.31), channel_id=1, source_target_pairs={{0,1},{1,2},{2,3},{3,0},{4,5},{5,6},{6,7},{7,4},{8,9},{9,10},{10,1... | collective-permute-start | bytes 24968 | tf_op jit(solution)/shard_map/ppermute | solution.py:20
  209.8 116.4 %collective-permute-start.24 = (f32[16,1,128]{2,0,1:T(8,128)S(1)}, f32[16,1,128]{2,0,1:T(8,128)S(1)}, u32[]{:S(2)}, u32[]{:S(2)}) collective-permute-start(f32[16,1,128]{2,0,1:T(8,128)S(1)} %get-tuple-element.62), channel_id=1, source_target_pairs={{4,0},{8,4},{12,8},{16,12},{20,16},{24,20},{28,24},{0,28},{5,1},{9... | collective-permute-start | bytes 24584 | tf_op jit(solution)/shard_map/ppermute | solution.py:22
  211.8 50.7 %collective-permute-start.25 = (f32[16,1,128]{2,0,1:T(8,128)S(1)}, f32[16,1,128]{2,0,1:T(8,128)S(1)}, u32[]{:S(2)}, u32[]{:S(2)}) collective-permute-start(f32[16,1,128]{2,0,1:T(8,128)S(1)} %get-tuple-element.63), channel_id=1, source_target_pairs={{0,4},{4,8},{8,12},{12,16},{16,20},{20,24},{24,28},{28,0},{1,5},{5... | collective-permute-start | bytes 24584 | tf_op jit(solution)/shard_map/ppermute | solution.py:20
  269.4 7.4 %collective-permute-start.19 = (f32[16,130,1]{1,0,2:T(8,128)S(1)}, f32[16,130,1]{1,0,2:T(8,128)S(1)}, u32[]{:S(2)}, u32[]{:S(2)}) collective-permute-start(f32[16,130,1]{1,0,2:T(8,128)S(1)} %copy.35), channel_id=1, source_target_pairs={{0,1},{1,2},{2,3},{3,0},{4,5},{5,6},{6,7},{7,4},{8,9},{9,10},{10,1... | collective-permute-start | bytes 24968 | tf_op jit(solution)/shard_map/ppermute | solution.py:20
  270.6 4.5 collective-permute-start.18
  323.5 4.1 collective-permute-start.20
  323.6 4.1 collective-permute-start.21
  331.7 17.0 %collective-permute-start.22 = (f32[16,132,2]{1,0,2:T(8,128)S(1)}, f32[16,132,2]{1,0,2:T(8,128)S(1)}, u32[]{:S(2)}, u32[]{:S(2)}) collective-permute-start(f32[16,132,2]{1,0,2:T(8,128)S(1)} %copy.37), channel_id=1, source_target_pairs={{0,1},{1,2},{2,3},{3,0},{4,5},{5,6},{6,7},{7,4},{8,9},{9,10},{10,1... | collective-permute-start | bytes 50696 | tf_op jit(solution)/shard_map/ppermute | solution.py:20
  333.8 14.0 %collective-permute-start.23 = (f32[16,132,2]{1,0,2:T(8,128)S(1)}, f32[16,132,2]{1,0,2:T(8,128)S(1)}, u32[]{:S(2)}, u32[]{:S(2)}) collective-permute-start(f32[16,132,2]{1,0,2:T(8,128)S(1)} %copy.38), channel_id=1, source_target_pairs={{1,0},{2,1},{3,2},{0,3},{5,4},{6,5},{7,6},{4,7},{9,8},{10,9},{11,1... | collective-permute-start | bytes 50696 | tf_op jit(solution)/shard_map/ppermute | solution.py:22
  340.0 6.1 %collective-permute-start.27 = (f32[16,130,1]{1,0,2:T(8,128)S(1)}, f32[16,130,1]{1,0,2:T(8,128)S(1)}, u32[]{:S(2)}, u32[]{:S(2)}) collective-permute-start(f32[16,130,1]{1,0,2:T(8,128)S(1)} %copy.50), channel_id=1, source_target_pairs={{0,1},{1,2},{2,3},{3,0},{4,5},{5,6},{6,7},{7,4},{8,9},{9,10},{10,1... | collective-permute-start | bytes 24968 | tf_op jit(solution)/shard_map/ppermute | solution.py:20
  367.6 5.6 %collective-permute-start.31 = (f32[16,130,1]{1,0,2:T(8,128)S(1)}, f32[16,130,1]{1,0,2:T(8,128)S(1)}, u32[]{:S(2)}, u32[]{:S(2)}) collective-permute-start(f32[16,130,1]{1,0,2:T(8,128)S(1)} %copy.54), channel_id=1, source_target_pairs={{0,1},{1,2},{2,3},{3,0},{4,5},{5,6},{6,7},{7,4},{8,9},{9,10},{10,1... | collective-permute-start | bytes 24968 | tf_op jit(solution)/shard_map/ppermute | solution.py:20
  387.3 4.1 collective-permute-start.34
  389.2 5.7 %collective-permute-start.35 = (f32[16,130,1]{1,0,2:T(8,128)S(1)}, f32[16,130,1]{1,0,2:T(8,128)S(1)}, u32[]{:S(2)}, u32[]{:S(2)}) collective-permute-start(f32[16,130,1]{1,0,2:T(8,128)S(1)} %copy.58), channel_id=1, source_target_pairs={{0,1},{1,2},{2,3},{3,0},{4,5},{5,6},{6,7},{7,4},{8,9},{9,10},{10,1... | collective-permute-start | bytes 24968 | tf_op jit(solution)/shard_map/ppermute | solution.py:20
  410.9 5.6 %collective-permute-start.39 = (f32[16,130,1]{1,0,2:T(8,128)S(1)}, f32[16,130,1]{1,0,2:T(8,128)S(1)}, u32[]{:S(2)}, u32[]{:S(2)}) collective-permute-start(f32[16,130,1]{1,0,2:T(8,128)S(1)} %copy.62), channel_id=1, source_target_pairs={{0,1},{1,2},{2,3},{3,0},{4,5},{5,6},{6,7},{7,4},{8,9},{9,10},{10,1... | collective-permute-start | bytes 24968 | tf_op jit(solution)/shard_map/ppermute | solution.py:20
  430.6 5.2 %collective-permute-start.42 = (f32[16,130,1]{1,0,2:T(8,128)S(1)}, f32[16,130,1]{1,0,2:T(8,128)S(1)}, u32[]{:S(2)}, u32[]{:S(2)}) collective-permute-start(f32[16,130,1]{1,0,2:T(8,128)S(1)} %copy.64), channel_id=1, source_target_pairs={{1,0},{2,1},{3,2},{0,3},{5,4},{6,5},{7,6},{4,7},{9,8},{10,9},{11,1... | collective-permute-start | bytes 24968 | tf_op jit(solution)/shard_map/ppermute | solution.py:22
  432.5 5.6 %collective-permute-start.43 = (f32[16,130,1]{1,0,2:T(8,128)S(1)}, f32[16,130,1]{1,0,2:T(8,128)S(1)}, u32[]{:S(2)}, u32[]{:S(2)}) collective-permute-start(f32[16,130,1]{1,0,2:T(8,128)S(1)} %copy.66), channel_id=1, source_target_pairs={{0,1},{1,2},{2,3},{3,0},{4,5},{5,6},{6,7},{7,4},{8,9},{9,10},{10,1... | collective-permute-start | bytes 24968 | tf_op jit(solution)/shard_map/ppermute | solution.py:20
  (35 other events, 158.8 us)
where the time goes:
time: 496 us; the launch traced here: 487 us
  blocking collectives  230 us (46%)
  local copies, waits for them, and re-layouts  88.9 us (18%)
  starting transfers between devices  74.5 us (15%)
  other arithmetic  50 us (10%)
  waiting for transfers between devices  35.4 us (7%)
  matrix products  6.08 us (1%)
    psum x5, blocking collectives, trial_shift(): return lax.psum(jnp.sum(trial, axis=(1, 2)), ('gx', 'gy')) / cells  192 us
    ppermute x22, starting transfers between devices, padded_2(): lax.ppermute(head, axis, [((i + 1) % count, i) for i in range(count)])  56.4 us
    psum x1, blocking collectives, class_mass(): return lax.psum(jnp.sum(density, axis=(1, 2)), ('gx', 'gy')) / cells  38.7 us
    slice x23, local copies, waits for them, and re-layouts, padded_2(): head = lax.slice_in_dim(cells, 0, width, axis=dim)  35.2 us
    ppermute x22, waiting for transfers between devices, padded_2(): lax.ppermute(tail, axis, [(i, (i + 1) % count) for i in range(count)])  30.8 us
    ppermute x22, starting transfers between devices, padded_2(): lax.ppermute(tail, axis, [(i, (i + 1) % count) for i in range(count)])  18.1 us
    ppermute x11, local copies, waits for them, and re-layouts, padded_2(): lax.ppermute(tail, axis, [(i, (i + 1) % count) for i in range(count)])  17.9 us
    add x4, other arithmetic, fp_step(): c_xp * padded[:, 2:, 1:-1] + c_xm * padded[:, :-2, 1:-1]  17.8 us
  transfers between devices with their start and end apart: 44, of which 24 were waited for; matrix products, arithmetic and copies ran while one was open for 11% of the time, Pallas kernels for 0%

commit v1 on v0

v1 whole, which is shorter than its diff:
```python
import functools

import jax
import jax.numpy as jnp
from jax import lax
from jax.experimental import pallas as pl
from jax.experimental.pallas import tpu as pltpu
from jax.sharding import PartitionSpec as P

MESH = pl.DeviceIdType.MESH
SWEEPS = 5
THETA = 2.0
PAD = 8
CHUNK = 32
UNROLL = 2


def kernel(
    nx, ny,
    cost_hbm, dens_hbm, coupling,
    trial_hbm, fresh_hbm, means,
    src, u, a, b, d0, d1, cxp, cxm, cyp, cym,
    xs, xr, ps, pr, xs2, xr2, ps2, pr2, edge, edge2,
    ar_out, ar_in, lam_tab,
    in_sem, out_sem, hs_sem, hr_sem, as_sem, ar_sem,
):
    classes, rows, cols = cost_hbm.shape
    n = nx * ny
    cells = float(n * rows * cols)
    gx, gy = lax.axis_index("gx"), lax.axis_index("gy")
    me = gx * ny + gy
    up, down = lax.rem(gx + nx - 1, nx), lax.rem(gx + 1, nx)
    left, right = lax.rem(gy + ny - 1, ny), lax.rem(gy + 1, ny)

    def at(x, y):
        return {"gx": x, "gy": y}

    def device(d):
        t = lax.rem(me + d, n)
        return at(t // ny, lax.rem(t, ny))

    load_d = pltpu.make_async_copy(dens_hbm, d0.at[:, pl.ds(PAD, rows), :], in_sem.at[0])
    load_c = pltpu.make_async_copy(cost_hbm, src, in_sem.at[1])
    load_d.start()
    load_c.start()

    barrier = pltpu.get_barrier_semaphore()

    def greet(d, carry):
        pl.semaphore_signal(barrier, inc=1, device_id=device(d), device_id_type=MESH)
        return carry

    lax.fori_loop(1, n, greet, 0)

    lane = lax.broadcasted_iota(jnp.int32, (1, cols), 1)
    lane_c = lax.broadcasted_iota(jnp.int32, (CHUNK, cols), 1)

    def geometry(w):
        span = 2 * w * classes
        return span, rows // (cols // span)

    def pack(ref, t, k, r0, w):
        span, block = geometry(w)
        p = span * (r0 // block) + 2 * w * k
        q = r0 % block
        turned = pltpu.roll(t, p + w, 1)
        mine = (lane_c >= p) & (lane_c < p + 2 * w)
        ref[q:q + CHUNK, :] = jnp.where(mine, turned, ref[q:q + CHUNK, :])

    def unpack(ref, k, r0, w):
        span, block = geometry(w)
        p = span * (r0 // block) + 2 * w * k
        q = r0 % block
        return pltpu.roll(ref[q:q + CHUNK, :], lax.rem(2 * cols - p, cols), 1)

    def halo_copies(e, w):
        sx, rx, sp, rp = (xs.at[e], xr.at[e], ps.at[e], pr.at[e]) if w == 1 else (xs2, xr2, ps2, pr2)
        plan = (
            (sx.at[0], rx.at[1], at(up, gy)),
            (sx.at[1], rx.at[0], at(down, gy)),
            (sp, rp.at[0], at(gx, right)),
            (sp, rp.at[1], at(gx, left)),
        )
        return [
            pltpu.make_async_remote_copy(
                src_ref=s, dst_ref=r, send_sem=hs_sem.at[e, i], recv_sem=hr_sem.at[e, i],
                device_id=dev, device_id_type=MESH,
            )
            for i, (s, r, dev) in enumerate(plan)
        ]

    def send_halo(e, w):
        copies = halo_copies(e, w)
        for c in copies:
            c.start()
        return copies

    def take_halo(copies, e, w, field):
        for c in copies:
            c.wait_recv()
        rx, rp, ed = (xr.at[e], pr.at[e], edge) if w == 1 else (xr2, pr2, edge2)
        for k in range(classes):
            for j in range(w):
                field[k, PAD - w + j:PAD - w + j + 1, :] = rx[0, j, k:k + 1, :]
                field[k, PAD + rows + j:PAD + rows + j + 1, :] = rx[1, j, k:k + 1, :]
        size = ed.shape[0]
        lanes = lax.broadcasted_iota(jnp.int32, (size, cols), 1)
        ed[...] = jnp.where(
            lax.rem(lanes, 2 * w) < w, rp[0], pltpu.roll(rp[1], cols - 2 * w, 1)
        )

    def edge_rows(ref, field, k, w):
        for j in range(w):
            ref[0, j, pl.ds(k, 1), :] = field[k, PAD + j:PAD + j + 1, :]
            ref[1, j, pl.ds(k, 1), :] = field[k, PAD + rows - w + j:PAD + rows - w + j + 1, :]

    def send_sums(s, row):
        ar_out[s] = row

        def send(d, carry):
            pltpu.make_async_remote_copy(
                src_ref=ar_out.at[s], dst_ref=ar_in.at[s, d - 1],
                send_sem=as_sem.at[s], recv_sem=ar_sem.at[s],
                device_id=device(d), device_id_type=MESH,
            ).start()
            return carry

        lax.fori_loop(1, n, send, 0)

    def take_sums(s, row):
        pltpu.make_async_copy(ar_in.at[s], ar_in.at[s], ar_sem.at[s]).wait()
        return row + jnp.sum(ar_in[s], axis=0)

    def fold(x):
        return jnp.sum(x.reshape(CHUNK // 8, 8, cols), axis=0)

    def put(row, place, part):
        return jnp.where(lane == place, jnp.sum(part, axis=(0, 1), keepdims=True), row)

    def spread(row):
        for k in range(classes):
            lam_tab[k] = jnp.broadcast_to(
                jnp.sum(jnp.where(lane == k, row, 0.0), axis=1, keepdims=True), (1, cols)
            )

    def offset_of(total, lam):
        return (total - lam * pltpu.roll(total, cols - classes, 1)) * (1.0 / cells)

    def each_class(body, init):
        return lax.fori_loop(0, classes, body, init, unroll=UNROLL)

    starts = range(0, rows, CHUNK)
    zero_row = jnp.zeros((1, cols), jnp.float32)

    load_d.wait()
    load_c.wait()

    def mix(i, carry):
        r = pl.multiple_of(i * 16, 16)
        parts = [d0[j, pl.ds(PAD + r, 16), :] for j in range(classes)]
        for k in range(classes):
            total = src[k, pl.ds(r, 16), :]
            for j in range(classes):
                total = total + coupling[k, j] * parts[j]
            src[k, pl.ds(r, 16), :] = total
        return carry

    lax.fori_loop(0, rows // 16, mix, 0)

    def first(k, row):
        total = jnp.zeros((8, cols), jnp.float32)
        for r0 in starts:
            t = src[k, r0:r0 + CHUNK, :] * 0.5
            u[k, PAD + r0:PAD + r0 + CHUNK, :] = t
            pack(ps.at[1], t, k, r0, 1)
            pack(ps.at[0], d0[k, PAD + r0:PAD + r0 + CHUNK, :], k, r0, 1)
            total = total + fold(t)
        edge_rows(xs.at[1], u, k, 1)
        edge_rows(xs.at[0], d0, k, 1)
        return put(row, k, total)

    row = each_class(first, zero_row)
    pl.semaphore_wait(barrier, n - 1)
    copies = send_halo(1, 1)
    send_sums(0, row)
    dens_copies = send_halo(0, 1)
    sent = [copies, dens_copies]
    lam = zero_row
    own = row

    def neighbours(field, ed, k, r0):
        lo = PAD + r0
        mid = field[k, lo:lo + CHUNK, :]
        xp = field[k, lo + 1:lo + 1 + CHUNK, :]
        xm = field[k, lo - 1:lo - 1 + CHUNK, :]
        side = unpack(ed, k, r0, 1)
        yp = jnp.where(lane_c == cols - 1, side, pltpu.roll(mid, cols - 1, 1))
        ym = jnp.where(lane_c == 0, side, pltpu.roll(mid, 1, 1))
        return xp, xm, yp, ym

    def linear(k, row):
        sum_a = jnp.zeros((8, cols), jnp.float32)
        sum_b = jnp.zeros((8, cols), jnp.float32)
        for r0 in starts:
            xp, xm, yp, ym = neighbours(u, edge, k, r0)
            px = jnp.abs(xp - xm) * 0.5
            py = jnp.abs(yp - ym) * 0.5
            sx, sy = xp + xm, yp + ym
            inv = 1.0 / (2.0 + px + py)
            gain = (sx + sy) + px * (sx - px) + py * (sy - py)
            at_a = (src[k, r0:r0 + CHUNK, :] + 0.5 * gain) * inv
            a[k, r0:r0 + CHUNK, :] = at_a
            b[k, r0:r0 + CHUNK, :] = inv
            sum_a = sum_a + fold(at_a)
            sum_b = sum_b + fold(inv)
        return put(put(row, k, sum_a), classes + k, sum_b)

    for s in range(1, SWEEPS):
        take_halo(copies, s, 1, u)
        row = each_class(linear, zero_row)
        send_sums(s, row)
        total = take_sums(s - 1, own)
        own = row
        offset = offset_of(total, lam)
        lam = THETA * offset
        spread(lam)
        last = s == SWEEPS - 1
        w = 2 if last else 1
        sp, sx = (ps2, xs2) if last else (ps.at[s + 1], xs.at[s + 1])

        def finish(k, carry):
            scale = lam_tab[k]
            for r0 in starts:
                t = a[k, r0:r0 + CHUNK, :] - scale * b[k, r0:r0 + CHUNK, :]
                u[k, PAD + r0:PAD + r0 + CHUNK, :] = t
                pack(sp, t, k, r0, w)
            edge_rows(sx, u, k, w)
            return carry

        each_class(finish, 0)
        copies = send_halo(s + 1, w)
        sent.append(copies)

    out_t = pltpu.make_async_copy(u.at[:, pl.ds(PAD, rows), :], trial_hbm, out_sem.at[0])
    out_t.start()
    take_halo(copies, SWEEPS, 2, u)
    take_halo(dens_copies, 0, 1, d0)

    def flow(field, into, e, c, d, k, r0):
        xp, xm, yp, ym = neighbours(field, edge, k, r0)
        f = c[0] * xp + c[1] * xm + c[2] * yp + c[3] * ym
        into[k, PAD + r0:PAD + r0 + CHUNK, :] = f
        if e is not None:
            pack(ps.at[e], f, k, r0, 1)
            return d
        return d + fold(f)

    base = SWEEPS + 1

    def weigh(k, carry):
        for r0 in starts:
            lo = PAD + r0
            mid = u[k, lo:lo + CHUNK, :]
            xp = u[k, lo + 1:lo + 1 + CHUNK, :]
            xm = u[k, lo - 1:lo - 1 + CHUNK, :]
            xpp = u[k, lo + 2:lo + 2 + CHUNK, :]
            xmm = u[k, lo - 2:lo - 2 + CHUNK, :]
            side = unpack(edge2, k, r0, 2)
            ypp = jnp.where(lane_c >= cols - 2, side, pltpu.roll(mid, cols - 2, 1))
            ymm = jnp.where(lane_c < 2, side, pltpu.roll(mid, 2, 1))
            yp = jnp.where(lane_c == cols - 1, pltpu.roll(side, 1, 1), pltpu.roll(mid, cols - 1, 1))
            ym = jnp.where(lane_c == 0, pltpu.roll(side, cols - 1, 1), pltpu.roll(mid, 1, 1))
            half = 0.5 / (2.0 + 0.5 * (jnp.abs(xp - xm) + jnp.abs(yp - ym)))
            c = [half * (1.0 + jnp.maximum(far - mid, 0.0)) for far in (xpp, xmm, ypp, ymm)]
            for ref, v in zip((cxp, cxm, cyp, cym), c):
                ref[k, r0:r0 + CHUNK, :] = v
            flow(d0, d1, base, c, None, k, r0)
        edge_rows(xs.at[base], d1, k, 1)
        return carry

    each_class(weigh, 0)
    copies = send_halo(base, 1)
    sent.append(copies)

    field, into = d1, d0
    for s in range(1, SWEEPS):
        take_halo(copies, base + s - 1, 1, field)
        last = s == SWEEPS - 1
        e = None if last else base + s

        def sweep(k, row):
            total = jnp.zeros((8, cols), jnp.float32)
            for r0 in starts:
                c = [ref[k, r0:r0 + CHUNK, :] for ref in (cxp, cxm, cyp, cym)]
                total = flow(field, into, e, c, total, k, r0)
            if last:
                return put(row, k, total)
            edge_rows(xs.at[e], into, k, 1)
            return row

        row = each_class(sweep, zero_row)
        if not last:
            copies = send_halo(e, 1)
            sent.append(copies)
        field, into = into, field

    send_sums(SWEEPS, row)
    out_f = pltpu.make_async_copy(field.at[:, pl.ds(PAD, rows), :], fresh_hbm, out_sem.at[1])
    out_f.start()
    total = take_sums(SWEEPS - 1, own)
    means[0:1, :] = offset_of(total, lam)
    for copies in sent:
        for c in copies:
            c.wait_send()
    total = take_sums(SWEEPS, row)
    means[1:2, :] = total * (1.0 / cells)
    for s in range(SWEEPS + 1):
        pltpu.make_async_copy(ar_in.at[s], ar_in.at[s], as_sem.at[s]).wait()
    out_t.wait()
    out_f.wait()


def shards(cost, density_start, coupling):
    nx, ny = lax.axis_size("gx"), lax.axis_size("gy")
    classes, rows, cols = cost.shape
    n = nx * ny
    f32 = jnp.float32
    full = pltpu.VMEM((classes, rows, cols), f32)
    padded = pltpu.VMEM((classes, rows + 2 * PAD, cols), f32)
    slots = 2 * SWEEPS
    block = rows * 2 * classes // cols
    trial, fresh, means = pl.pallas_call(
        functools.partial(kernel, nx, ny),
        out_shape=(
            jax.ShapeDtypeStruct(cost.shape, f32),
            jax.ShapeDtypeStruct(cost.shape, f32),
            jax.ShapeDtypeStruct((2, cols), f32),
        ),
        in_specs=[
            pl.BlockSpec(memory_space=pl.ANY),
            pl.BlockSpec(memory_space=pl.ANY),
            pl.BlockSpec(memory_space=pltpu.SMEM),
        ],
        out_specs=(
            pl.BlockSpec(memory_space=pl.ANY),
            pl.BlockSpec(memory_space=pl.ANY),
            pl.BlockSpec(memory_space=pltpu.VMEM),
        ),
        scratch_shapes=[
            full, padded, full, full, padded, padded, full, full, full, full,
            pltpu.VMEM((slots, 2, 1, classes, cols), f32),
            pltpu.VMEM((slots, 2, 1, classes, cols), f32),
            pltpu.VMEM((slots, block, cols), f32),
            pltpu.VMEM((slots, 2, block, cols), f32),
            pltpu.VMEM((2, 2, classes, cols), f32),
            pltpu.VMEM((2, 2, classes, cols), f32),
            pltpu.VMEM((2 * block, cols), f32),
            pltpu.VMEM((2, 2 * block, cols), f32),
            pltpu.VMEM((block, cols), f32),
            pltpu.VMEM((2 * block, cols), f32),
            pltpu.VMEM((SWEEPS + 1, 1, cols), f32),
            pltpu.VMEM((SWEEPS + 1, n - 1, 1, cols), f32),
            pltpu.VMEM((classes, 1, cols), f32),
            pltpu.SemaphoreType.DMA((2,)),
            pltpu.SemaphoreType.DMA((2,)),
            pltpu.SemaphoreType.DMA((slots, 4)),
            pltpu.SemaphoreType.DMA((slots, 4)),
            pltpu.SemaphoreType.DMA((SWEEPS + 1,)),
            pltpu.SemaphoreType.DMA((SWEEPS + 1,)),
        ],
        compiler_params=pltpu.CompilerParams(
            collective_id=0, has_side_effects=True, vmem_limit_bytes=48 * 1024 * 1024
        ),
    )(cost, density_start, coupling)
    offset = means[0, :classes]
    mass = means[1, :classes]
    value = trial - offset[:, None, None]
    density = fresh / mass[:, None, None]
    return value, density, THETA * offset


def solution(mesh):
    placed = P(None, "gx", "gy")
    return jax.shard_map(
        shards,
        mesh=mesh,
        in_specs=(placed, placed, P()),
        out_specs=(placed, placed, P()),
        check_vma=False,
    )
```

time: 496 us -> 86.7 us (0.17); the launches traced: 487 us -> 86.4 us
  blocking collectives: 230 us -> 0 us
  local copies, waits for them, and re-layouts: 88.9 us -> 3.14 us
  Pallas kernels: 0 us -> 80.7 us
  starting transfers between devices: 74.5 us -> 0 us
  other arithmetic: 50 us -> 1.99 us
  waiting for transfers between devices: 35.4 us -> 0 us
  matrix products: 6.08 us -> 0 us
    psum x6 -> x0, blocking collectives: 230 us -> none  [the longest x5 192 us: trial_shift(): return lax.psum(jnp.sum(trial, axis=(1, 2)), ('gx', 'gy')) / cells]
    pallas_call x0 -> x1, Pallas kernels: none -> 80.7 us  [shards(): pl.pallas_call(functools.partial(kernel, nx, ny), out_shape=(jax.ShapeDty...]
    ppermute x44 -> x0, starting transfers between devices: 74.5 us -> none  [the longest x22 56.4 us: padded_2(): lax.ppermute(head, axis, [((i + 1) % count, i) for i in range(count)])]
    slice x43 -> x0, local copies, waits for them, and re-layouts: 49.7 us -> none  [the longest x23 35.2 us: padded_2(): head = lax.slice_in_dim(cells, 0, width, axis=dim)]
    ppermute x44 -> x0, waiting for transfers between devices: 35.4 us -> none  [the longest x22 30.8 us: padded_2(): lax.ppermute(tail, axis, [(i, (i + 1) % count) for i in range(count)])]
    ppermute x22 -> x0, local copies, waits for them, and re-layouts: 32.6 us -> none  [the longest x11 17.9 us: padded_2(): lax.ppermute(tail, axis, [(i, (i + 1) % count) for i in range(count)])]
    add x7 -> x0, other arithmetic: 20.3 us -> none  [the longest x4 17.8 us: fp_step(): c_xp * padded[:, 2:, 1:-1] + c_xm * padded[:, :-2, 1:-1]]
    reduce_sum x5 -> x0, other arithmetic: 19.8 us -> none  [the longest x4 14.5 us: trial_shift(): return lax.psum(jnp.sum(trial, axis=(1, 2)), ('gx', 'gy')) / cells]
  transfers between devices with their start and end apart: 44 -> 0, of which waited for: 24 -> 0; matrix products, arithmetic and copies ran while one was open for 11% -> 0% of each run, Pallas kernels for 0% -> 0%
where the time goes in v1:
time: 86.7 us; the launch traced here: 86.4 us
  Pallas kernels  80.7 us (93%)
  local copies, waits for them, and re-layouts  3.14 us (4%)
  other arithmetic  1.99 us (2%)
    pallas_call x1, Pallas kernels, shards(): pl.pallas_call(functools.partial(kernel, nx, ny), out_shape=(jax.ShapeDty...  80.7 us
    unnamed x6, local copies, waits for them, and re-layouts  3.14 us

profile of v1, /device:TPU:0, one launch (start us, length us, event | category | flops | bytes accessed | tf_op | source)
XLA Modules:
  0.0 86.4 jit_solution(11491379608248456476)
XLA Ops:
  0.6 0.0 copy-start
  0.6 1.2 %copy-done = f32[16,128,128]{2,1,0:T(8,128)S(1)} copy-done((f32[16,128,128]{2,1,0:T(8,128)S(1)}, f32[16,128,128]{2,1,0:T(8,128)}, u32[]{:S(2)}) %copy-start) | copy-done | bytes 1048600
  1.9 0.0 copy-start.1
  1.9 1.2 %copy-done.1 = f32[16,128,128]{2,1,0:T(8,128)S(1)} copy-done((f32[16,128,128]{2,1,0:T(8,128)S(1)}, f32[16,128,128]{2,1,0:T(8,128)}, u32[]{:S(2)}) %copy-start.1) | copy-done | bytes 1048600
  3.1 0.0 copy-start.2
  3.1 0.7 copy-done.2
  3.8 80.7 %shard_map.58 = (f32[16,128,128]{2,1,0:T(8,128)S(1)}, f32[16,128,128]{2,1,0:T(8,128)S(1)}, f32[2,128]{1,0:T(2,128)S(1)}) custom-call(f32[16,128,128]{2,1,0:T(8,128)S(1)} %copy-done, f32[16,128,128]{2,1,0:T(8,128)S(1)} %copy-done.1, f32[16,16]{1,0:T(8,128)S(1)} %copy-done.2), custom_call_target="tpu_custom_call" | custom-call | tf_op jit(solution)/shard_map/pallas_call | solution.py:332
  84.4 0.5 broadcast_multiply_fusion
  85.0 1.5 %broadcast_divide_fusion = (f32[16,128,128]{2,1,0:T(8,128)}, f32[16,128,128]{2,1,0:T(8,128)}) fusion(f32[16,128,128]{2,1,0:T(8,128)S(1)} %get-tuple-element.8, f32[16]{0:T(128)S(1)} %get-tuple-element.9, f32[16,128,128]{2,1,0:T(8,128)S(1)} %get-tuple-element.6, f32[16]{0:T(128)S(1)} %get-tuple-element.10), kind=kLoop, calls=%fused_computation | loop fusion | flops 524288 | bytes 4194432 | tf_op jit(solution)/shard_map/div | solution.py:378
  (1 shorter events, 0.0 us)
Async XLA Ops:
  0.6 1.2 %copy-start = (f32[16,128,128]{2,1,0:T(8,128)S(1)}, f32[16,128,128]{2,1,0:T(8,128)}, u32[]{:S(2)}) copy-start(f32[16,128,128]{2,1,0:T(8,128)} %cost_hbm.1) | copy-start | bytes 3145732
  1.9 1.2 %copy-start.1 = (f32[16,128,128]{2,1,0:T(8,128)S(1)}, f32[16,128,128]{2,1,0:T(8,128)}, u32[]{:S(2)}) copy-start(f32[16,128,128]{2,1,0:T(8,128)} %dens_hbm.1) | copy-start | bytes 3145732
  3.1 0.7 copy-start.2

commit v2 on v1

--- a/solution.py
+++ b/solution.py
@@ -20,24 +20,22 @@
     cost_hbm, dens_hbm, coupling,
     trial_hbm, fresh_hbm, means,
     src, u, a, b, d0, d1, cxp, cxm, cyp, cym,
-    xs, xr, ps, pr, xs2, xr2, ps2, pr2, edge, edge2,
-    ar_out, ar_in, lam_tab,
-    in_sem, out_sem, hs_sem, hr_sem, as_sem, ar_sem,
+    xs, xr, ps, pr, xs2, xr2, ps2, pr2, edge, edge2, edge3,
+    arx_out, arx_in, ary_out, ary_in, lam_tab,
+    in_sem, out_sem, hs_sem, hr_sem, axs_sem, axr_sem, ays_sem, ayr_sem,
 ):
     classes, rows, cols = cost_hbm.shape
     n = nx * ny
     cells = float(n * rows * cols)
     gx, gy = lax.axis_index("gx"), lax.axis_index("gy")
-    me = gx * ny + gy
     up, down = lax.rem(gx + nx - 1, nx), lax.rem(gx + 1, nx)
     left, right = lax.rem(gy + ny - 1, ny), lax.rem(gy + 1, ny)
 
     def at(x, y):
         return {"gx": x, "gy": y}
 
-    def device(d):
-        t = lax.rem(me + d, n)
-        return at(t // ny, lax.rem(t, ny))
+    peers_x = [at(lax.rem(gx + d, nx), gy) for d in range(1, nx)]
+    peers_y = [at(gx, lax.rem(gy + d, ny)) for d in range(1, ny)]
 
     load_d = pltpu.make_async_copy(dens_hbm, d0.at[:, pl.ds(PAD, rows), :], in_sem.at[0])
     load_c = pltpu.make_async_copy(cost_hbm, src, in_sem.at[1])
@@ -46,11 +44,8 @@
 
     barrier = pltpu.get_barrier_semaphore()
 
-    def greet(d, carry):
-        pl.semaphore_signal(barrier, inc=1, device_id=device(d), device_id_type=MESH)
-        return carry
-
-    lax.fori_loop(1, n, greet, 0)
+    for peer in peers_x + peers_y:
+        pl.semaphore_signal(barrier, inc=1, device_id=peer, device_id_type=MESH)
 
     lane = lax.broadcasted_iota(jnp.int32, (1, cols), 1)
     lane_c = lax.broadcasted_iota(jnp.int32, (CHUNK, cols), 1)
@@ -114,22 +109,27 @@
             ref[0, j, pl.ds(k, 1), :] = field[k, PAD + j:PAD + j + 1, :]
             ref[1, j, pl.ds(k, 1), :] = field[k, PAD + rows - w + j:PAD + rows - w + j + 1, :]
 
+    def send_part(s, row, peers, out, into, send_sem, recv_sem):
+        out[s] = row
+        for i, peer in enumerate(peers):
+            pltpu.make_async_remote_copy(
+                src_ref=out.at[s], dst_ref=into.at[s, i],
+                send_sem=send_sem.at[s], recv_sem=recv_sem.at[s],
+                device_id=peer, device_id_type=MESH,
+            ).start()
+
     def send_sums(s, row):
-        ar_out[s] = row
-
-        def send(d, carry):
-            pltpu.make_async_remote_copy(
-                src_ref=ar_out.at[s], dst_ref=ar_in.at[s, d - 1],
-                send_sem=as_sem.at[s], recv_sem=ar_sem.at[s],
-                device_id=device(d), device_id_type=MESH,
-            ).start()
-            return carry
-
-        lax.fori_loop(1, n, send, 0)
-
-    def take_sums(s, row):
-        pltpu.make_async_copy(ar_in.at[s], ar_in.at[s], ar_sem.at[s]).wait()
-        return row + jnp.sum(ar_in[s], axis=0)
+        send_part(s, row, peers_x, arx_out, arx_in, axs_sem, axr_sem)
+
+    def pass_sums(s, row):
+        pltpu.make_async_copy(arx_in.at[s], arx_in.at[s], axr_sem.at[s]).wait()
+        part = row + jnp.sum(arx_in[s], axis=0)
+        send_part(s, part, peers_y, ary_out, ary_in, ays_sem, ayr_sem)
+        return part
+
+    def take_sums(s, part):
+        pltpu.make_async_copy(ary_in.at[s], ary_in.at[s], ayr_sem.at[s]).wait()
+        return part + jnp.sum(ary_in[s], axis=0)
 
     def fold(x):
         return jnp.sum(x.reshape(CHUNK // 8, 8, cols), axis=0)
@@ -180,13 +180,13 @@
         return put(row, k, total)
 
     row = each_class(first, zero_row)
-    pl.semaphore_wait(barrier, n - 1)
+    pl.semaphore_wait(barrier, nx + ny - 2)
     copies = send_halo(1, 1)
     send_sums(0, row)
     dens_copies = send_halo(0, 1)
     sent = [copies, dens_copies]
     lam = zero_row
-    own = row
+    own = pass_sums(0, row)
 
     def neighbours(field, ed, k, r0):
         lo = PAD + r0
@@ -220,7 +220,6 @@
         row = each_class(linear, zero_row)
         send_sums(s, row)
         total = take_sums(s - 1, own)
-        own = row
         offset = offset_of(total, lam)
         lam = THETA * offset
         spread(lam)
@@ -240,11 +239,16 @@
         each_class(finish, 0)
         copies = send_halo(s + 1, w)
         sent.append(copies)
+        own = pass_sums(s, row)
 
     out_t = pltpu.make_async_copy(u.at[:, pl.ds(PAD, rows), :], trial_hbm, out_sem.at[0])
     out_t.start()
     take_halo(copies, SWEEPS, 2, u)
     take_halo(dens_copies, 0, 1, d0)
+    lanes2 = lax.broadcasted_iota(jnp.int32, edge2.shape, 1)
+    edge3[...] = jnp.where(
+        lax.rem(lanes2, 4) < 2, pltpu.roll(edge2[...], cols - 1, 1), pltpu.roll(edge2[...], 1, 1)
+    )
 
     def flow(field, into, e, c, d, k, r0):
         xp, xm, yp, ym = neighbours(field, edge, k, r0)
@@ -266,10 +270,11 @@
             xpp = u[k, lo + 2:lo + 2 + CHUNK, :]
             xmm = u[k, lo - 2:lo - 2 + CHUNK, :]
             side = unpack(edge2, k, r0, 2)
+            near = unpack(edge3, k, r0, 2)
             ypp = jnp.where(lane_c >= cols - 2, side, pltpu.roll(mid, cols - 2, 1))
             ymm = jnp.where(lane_c < 2, side, pltpu.roll(mid, 2, 1))
-            yp = jnp.where(lane_c == cols - 1, pltpu.roll(side, 1, 1), pltpu.roll(mid, cols - 1, 1))
-            ym = jnp.where(lane_c == 0, pltpu.roll(side, cols - 1, 1), pltpu.roll(mid, 1, 1))
+            yp = jnp.where(lane_c == cols - 1, near, pltpu.roll(mid, cols - 1, 1))
+            ym = jnp.where(lane_c == 0, near, pltpu.roll(mid, 1, 1))
             half = 0.5 / (2.0 + 0.5 * (jnp.abs(xp - xm) + jnp.abs(yp - ym)))
             c = [half * (1.0 + jnp.maximum(far - mid, 0.0)) for far in (xpp, xmm, ypp, ymm)]
             for ref, v in zip((cxp, cxm, cyp, cym), c):
@@ -307,15 +312,17 @@
     send_sums(SWEEPS, row)
     out_f = pltpu.make_async_copy(field.at[:, pl.ds(PAD, rows), :], fresh_hbm, out_sem.at[1])
     out_f.start()
+    part = pass_sums(SWEEPS, row)
     total = take_sums(SWEEPS - 1, own)
     means[0:1, :] = offset_of(total, lam)
     for copies in sent:
         for c in copies:
             c.wait_send()
-    total = take_sums(SWEEPS, row)
+    total = take_sums(SWEEPS, part)
     means[1:2, :] = total * (1.0 / cells)
     for s in range(SWEEPS + 1):
-        pltpu.make_async_copy(ar_in.at[s], ar_in.at[s], as_sem.at[s]).wait()
+        pltpu.make_async_copy(arx_in.at[s], arx_in.at[s], axs_sem.at[s]).wait()
+        pltpu.make_async_copy(ary_in.at[s], ary_in.at[s], ays_sem.at[s]).wait()
     out_t.wait()
     out_f.wait()
 
@@ -323,7 +330,6 @@
 def shards(cost, density_start, coupling):
     nx, ny = lax.axis_size("gx"), lax.axis_size("gy")
     classes, rows, cols = cost.shape
-    n = nx * ny
     f32 = jnp.float32
     full = pltpu.VMEM((classes, rows, cols), f32)
     padded = pltpu.VMEM((classes, rows + 2 * PAD, cols), f32)
@@ -358,8 +364,11 @@
             pltpu.VMEM((2, 2 * block, cols), f32),
             pltpu.VMEM((block, cols), f32),
             pltpu.VMEM((2 * block, cols), f32),
+            pltpu.VMEM((2 * block, cols), f32),
             pltpu.VMEM((SWEEPS + 1, 1, cols), f32),
-            pltpu.VMEM((SWEEPS + 1, n - 1, 1, cols), f32),
+            pltpu.VMEM((SWEEPS + 1, nx - 1, 1, cols), f32),
+            pltpu.VMEM((SWEEPS + 1, 1, cols), f32),
+            pltpu.VMEM((SWEEPS + 1, ny - 1, 1, cols), f32),
             pltpu.VMEM((classes, 1, cols), f32),
             pltpu.SemaphoreType.DMA((2,)),
             pltpu.SemaphoreType.DMA((2,)),
@@ -367,9 +376,11 @@
             pltpu.SemaphoreType.DMA((slots, 4)),
             pltpu.SemaphoreType.DMA((SWEEPS + 1,)),
             pltpu.SemaphoreType.DMA((SWEEPS + 1,)),
+            pltpu.SemaphoreType.DMA((SWEEPS + 1,)),
+            pltpu.SemaphoreType.DMA((SWEEPS + 1,)),
         ],
         compiler_params=pltpu.CompilerParams(
-            collective_id=0, has_side_effects=True, vmem_limit_bytes=48 * 1024 * 1024
+            collective_id=0, has_side_effects=True, vmem_limit_bytes=67043328
         ),
     )(cost, density_start, coupling)
     offset = means[0, :classes]

time: 86.7 us -> 85.2 us (0.983)
  local copies, waits for them, and re-layouts: 3.14 us -> 0.65 us
  other arithmetic: 1.99 us -> 3.53 us
    unnamed x6 -> x2, local copies, waits for them, and re-layouts: 3.14 us -> 0.65 us
    div x1, other arithmetic: 1.48 us -> 3.02 us  [shards(): density = fresh / mass[:, None, None]]
where the time goes in v2:
time: 85.2 us; the launch traced here: 84.9 us
  Pallas kernels  80.1 us (94%)
  other arithmetic  3.53 us (4%)
    pallas_call x1, Pallas kernels, shards(): pl.pallas_call(functools.partial(kernel, nx, ny), out_shape=(jax.ShapeDty...  80.1 us
    div x1, other arithmetic, shards(): density = fresh / mass[:, None, None]  3.02 us

profile of v2, /device:TPU:0, one launch (start us, length us, event | category | flops | bytes accessed | tf_op | source)
XLA Modules:
  0.0 84.9 jit_solution(4185459949378424375)
XLA Ops:
  0.6 80.1 %shard_map.58 = (f32[16,128,128]{2,1,0:T(8,128)}, f32[16,128,128]{2,1,0:T(8,128)}, f32[2,128]{1,0:T(2,128)}) custom-call(f32[16,128,128]{2,1,0:T(8,128)} %cost_hbm.1, f32[16,128,128]{2,1,0:T(8,128)} %dens_hbm.1, f32[16,16]{1,0:T(8,128)} %coupling.1), custom_call_target="tpu_custom_call" | custom-call | tf_op jit(solution)/shard_map/pallas_call | solution.py:338
  80.7 0.0 copy-start
  80.8 0.6 copy-done
  81.4 0.5 broadcast_multiply_fusion
  81.9 3.0 %broadcast_divide_fusion = (f32[16,128,128]{2,1,0:T(8,128)}, f32[16,128,128]{2,1,0:T(8,128)}) fusion(f32[16,128,128]{2,1,0:T(8,128)} %get-tuple-element.8, f32[16]{0:T(128)S(1)} %get-tuple-element.9, f32[16,128,128]{2,1,0:T(8,128)} %get-tuple-element.6, f32[16]{0:T(128)S(1)} %get-tuple-element.10), kind=kLoop, calls=%fused_computation | loop fusion | flops 524288 | bytes 4194432 | tf_op jit(solution)/shard_map/div | solution.py:389
  (1 shorter events, 0.0 us)
Async XLA Ops:
  80.7 0.7 copy-start

commit v3 on v2

v3 whole, which is shorter than its diff:
```python
import functools

import jax
import jax.numpy as jnp
from jax import lax
from jax.experimental import pallas as pl
from jax.experimental.pallas import tpu as pltpu
from jax.sharding import PartitionSpec as P

MESH = pl.DeviceIdType.MESH
SWEEPS = 5
THETA = 2.0
PAD = 8
CHUNK = 16
GROUPS = 2
UNROLL = 2


def kernel(
    nx, ny,
    cost_hbm, dens_hbm, coupling,
    trial_hbm, fresh_hbm, means,
    src, u, a, b, d0, d1, cxp, cxm, cyp, cym,
    xs, xr, ps, pr, xs2, xr2, ps2, pr2, edge, edge2, edge3,
    arx_out, arx_in, ary_out, ary_in, lam_tab,
    in_sem, out_sem, hs_sem, hr_sem, axs_sem, axr_sem, ays_sem, ayr_sem,
):
    classes, rows, cols = cost_hbm.shape
    n = nx * ny
    part_of = classes // GROUPS
    cells = float(n * rows * cols)
    gx, gy = lax.axis_index("gx"), lax.axis_index("gy")
    up, down = lax.rem(gx + nx - 1, nx), lax.rem(gx + 1, nx)
    left, right = lax.rem(gy + ny - 1, ny), lax.rem(gy + 1, ny)

    def at(x, y):
        return {"gx": x, "gy": y}

    peers_x = [at(lax.rem(gx + d, nx), gy) for d in range(1, nx)]
    peers_y = [at(gx, lax.rem(gy + d, ny)) for d in range(1, ny)]

    load_d = pltpu.make_async_copy(dens_hbm, d0.at[:, pl.ds(PAD, rows), :], in_sem.at[0])
    load_c = pltpu.make_async_copy(cost_hbm, src, in_sem.at[1])
    load_d.start()
    load_c.start()

    barrier = pltpu.get_barrier_semaphore()

    for peer in peers_x + peers_y:
        pl.semaphore_signal(barrier, inc=1, device_id=peer, device_id_type=MESH)

    lane = lax.broadcasted_iota(jnp.int32, (1, cols), 1)
    lane_c = lax.broadcasted_iota(jnp.int32, (CHUNK, cols), 1)

    def geometry(w):
        span = 2 * w * part_of
        return span, rows // (cols // span)

    def pack(ref, t, k, r0, w):
        span, block = geometry(w)
        p = span * (r0 // block) + 2 * w * lax.rem(k, part_of)
        q = r0 % block
        turned = pltpu.roll(t, p + w, 1)
        mine = (lane_c >= p) & (lane_c < p + 2 * w)
        ref[q:q + CHUNK, :] = jnp.where(mine, turned, ref[q:q + CHUNK, :])

    def unpack(ref, k, r0, w):
        span, block = geometry(w)
        p = span * (r0 // block) + 2 * w * lax.rem(k, part_of)
        q = r0 % block
        return pltpu.roll(ref[q:q + CHUNK, :], lax.rem(2 * cols - p, cols), 1)

    def halo_copies(e, w, g):
        e = e * GROUPS + g
        sx, rx, sp, rp = (xs.at[e], xr.at[e], ps.at[e], pr.at[e]) if w == 1 else (xs2.at[g], xr2.at[g], ps2.at[g], pr2.at[g])
        plan = (
            (sx.at[0], rx.at[1], at(up, gy)),
            (sx.at[1], rx.at[0], at(down, gy)),
            (sp, rp.at[0], at(gx, right)),
            (sp, rp.at[1], at(gx, left)),
        )
        return [
            pltpu.make_async_remote_copy(
                src_ref=s, dst_ref=r, send_sem=hs_sem.at[e, i], recv_sem=hr_sem.at[e, i],
                device_id=dev, device_id_type=MESH,
            )
            for i, (s, r, dev) in enumerate(plan)
        ]

    def send_halo(e, w, g):
        copies = halo_copies(e, w, g)
        for c in copies:
            c.start()
        return copies

    def take_halo(copies, e, w, field, g):
        e = e * GROUPS + g
        for c in copies:
            c.wait_recv()
        rx, rp, ed = (xr.at[e], pr.at[e], edge.at[g]) if w == 1 else (xr2.at[g], pr2.at[g], edge2.at[g])
        for i in range(part_of):
            k = g * part_of + i
            for j in range(w):
                field[k, PAD - w + j:PAD - w + j + 1, :] = rx[0, j, i:i + 1, :]
                field[k, PAD + rows + j:PAD + rows + j + 1, :] = rx[1, j, i:i + 1, :]
        size = ed.shape[0]
        lanes = lax.broadcasted_iota(jnp.int32, (size, cols), 1)
        ed[...] = jnp.where(
            lax.rem(lanes, 2 * w) < w, rp[0], pltpu.roll(rp[1], cols - 2 * w, 1)
        )

    def edge_rows(ref, field, k, w):
        i = lax.rem(k, part_of)
        for j in range(w):
            ref[0, j, pl.ds(i, 1), :] = field[k, PAD + j:PAD + j + 1, :]
            ref[1, j, pl.ds(i, 1), :] = field[k, PAD + rows - w + j:PAD + rows - w + j + 1, :]

    def send_part(s, row, peers, out, into, send_sem, recv_sem):
        out[s] = row
        for i, peer in enumerate(peers):
            pltpu.make_async_remote_copy(
                src_ref=out.at[s], dst_ref=into.at[s, i],
                send_sem=send_sem.at[s], recv_sem=recv_sem.at[s],
                device_id=peer, device_id_type=MESH,
            ).start()

    def send_sums(s, row):
        send_part(s, row, peers_x, arx_out, arx_in, axs_sem, axr_sem)

    def pass_sums(s, row):
        pltpu.make_async_copy(arx_in.at[s], arx_in.at[s], axr_sem.at[s]).wait()
        part = row + jnp.sum(arx_in[s], axis=0)
        send_part(s, part, peers_y, ary_out, ary_in, ays_sem, ayr_sem)
        return part

    def take_sums(s, part):
        pltpu.make_async_copy(ary_in.at[s], ary_in.at[s], ayr_sem.at[s]).wait()
        return part + jnp.sum(ary_in[s], axis=0)

    def fold(x):
        return jnp.sum(x.reshape(CHUNK // 8, 8, cols), axis=0)

    def put(row, place, part):
        return jnp.where(lane == place, jnp.sum(part, axis=(0, 1), keepdims=True), row)

    def spread(row, g):
        for k in range(g * part_of, (g + 1) * part_of):
            lam_tab[k] = jnp.broadcast_to(
                jnp.sum(jnp.where(lane == k, row, 0.0), axis=1, keepdims=True), (1, cols)
            )

    def offset_of(total, lam):
        return (total - lam * pltpu.roll(total, cols - classes, 1)) * (1.0 / cells)

    def each_class(g, body, init):
        return lax.fori_loop(g * part_of, (g + 1) * part_of, body, init, unroll=UNROLL)

    starts = range(0, rows, CHUNK)
    zero_row = jnp.zeros((1, cols), jnp.float32)

    load_d.wait()
    load_c.wait()

    def mix(i, carry):
        r = pl.multiple_of(i * 16, 16)
        parts = [d0[j, pl.ds(PAD + r, 16), :] for j in range(classes)]
        for k in range(classes):
            total = src[k, pl.ds(r, 16), :]
            for j in range(classes):
                total = total + coupling[k, j] * parts[j]
            src[k, pl.ds(r, 16), :] = total
        return carry

    lax.fori_loop(0, rows // 16, mix, 0)

    def first(g, k, row):
        total = jnp.zeros((8, cols), jnp.float32)
        for r0 in starts:
            t = src[k, r0:r0 + CHUNK, :] * 0.5
            u[k, PAD + r0:PAD + r0 + CHUNK, :] = t
            pack(ps.at[GROUPS + g], t, k, r0, 1)
            pack(ps.at[g], d0[k, PAD + r0:PAD + r0 + CHUNK, :], k, r0, 1)
            total = total + fold(t)
        edge_rows(xs.at[GROUPS + g], u, k, 1)
        edge_rows(xs.at[g], d0, k, 1)
        return put(row, k, total)

    copies, dens_copies, rows_of, own, sent = {}, {}, {}, {}, []
    lam = {g: zero_row for g in range(GROUPS)}
    pending = []

    def settle():
        while pending:
            s, g = pending.pop(0)
            own[g] = pass_sums(s * GROUPS + g, rows_of[g])

    for g in range(GROUPS):
        rows_of[g] = each_class(g, functools.partial(first, g), zero_row)
        if g == 0:
            pl.semaphore_wait(barrier, nx + ny - 2)
        copies[g] = send_halo(1, 1, g)
        send_sums(g, rows_of[g])
        dens_copies[g] = send_halo(0, 1, g)
        sent += [copies[g], dens_copies[g]]
        pending.append((0, g))

    def neighbours(field, ed, k, r0):
        lo = PAD + r0
        mid = field[k, lo:lo + CHUNK, :]
        xp = field[k, lo + 1:lo + 1 + CHUNK, :]
        xm = field[k, lo - 1:lo - 1 + CHUNK, :]
        side = unpack(ed, k, r0, 1)
        yp = jnp.where(lane_c == cols - 1, side, pltpu.roll(mid, cols - 1, 1))
        ym = jnp.where(lane_c == 0, side, pltpu.roll(mid, 1, 1))
        return xp, xm, yp, ym

    def linear(g, k, row):
        sum_a = jnp.zeros((8, cols), jnp.float32)
        sum_b = jnp.zeros((8, cols), jnp.float32)
        for r0 in starts:
            xp, xm, yp, ym = neighbours(u, edge.at[g], k, r0)
            px = jnp.abs(xp - xm) * 0.5
            py = jnp.abs(yp - ym) * 0.5
            sx, sy = xp + xm, yp + ym
            inv = 1.0 / (2.0 + px + py)
            gain = (sx + sy) + px * (sx - px) + py * (sy - py)
            at_a = (src[k, r0:r0 + CHUNK, :] + 0.5 * gain) * inv
            a[k, r0:r0 + CHUNK, :] = at_a
            b[k, r0:r0 + CHUNK, :] = inv
            sum_a = sum_a + fold(at_a)
            sum_b = sum_b + fold(inv)
        return put(put(row, k, sum_a), classes + k, sum_b)

    for s in range(1, SWEEPS):
        last = s == SWEEPS - 1
        w = 2 if last else 1
        for g in range(GROUPS):
            take_halo(copies[g], s, 1, u, g)
            settle()
            row = each_class(g, functools.partial(linear, g), zero_row)
            send_sums(s * GROUPS + g, row)
            total = take_sums((s - 1) * GROUPS + g, own[g])
            lam[g] = THETA * offset_of(total, lam[g])
            spread(lam[g], g)
            rows_of[g] = row
            slot = (s + 1) * GROUPS + g
            sp, sx = (ps2.at[g], xs2.at[g]) if last else (ps.at[slot], xs.at[slot])

            def finish(k, carry):
                scale = lam_tab[k]
                for r0 in starts:
                    t = a[k, r0:r0 + CHUNK, :] - scale * b[k, r0:r0 + CHUNK, :]
                    u[k, PAD + r0:PAD + r0 + CHUNK, :] = t
                    pack(sp, t, k, r0, w)
                edge_rows(sx, u, k, w)
                return carry

            each_class(g, finish, 0)
            copies[g] = send_halo(s + 1, w, g)
            sent.append(copies[g])
            pending.append((s, g))

    out_t = pltpu.make_async_copy(u.at[:, pl.ds(PAD, rows), :], trial_hbm, out_sem.at[0])
    out_t.start()
    def flow(field, into, e, c, d, g, k, r0):
        xp, xm, yp, ym = neighbours(field, edge.at[g], k, r0)
        f = c[0] * xp + c[1] * xm + c[2] * yp + c[3] * ym
        into[k, PAD + r0:PAD + r0 + CHUNK, :] = f
        if e is not None:
            pack(ps.at[e * GROUPS + g], f, k, r0, 1)
            return d
        return d + fold(f)

    base = SWEEPS + 1

    def weigh(g, k, carry):
        for r0 in starts:
            lo = PAD + r0
            mid = u[k, lo:lo + CHUNK, :]
            xp = u[k, lo + 1:lo + 1 + CHUNK, :]
            xm = u[k, lo - 1:lo - 1 + CHUNK, :]
            xpp = u[k, lo + 2:lo + 2 + CHUNK, :]
            xmm = u[k, lo - 2:lo - 2 + CHUNK, :]
            side = unpack(edge2.at[g], k, r0, 2)
            near = unpack(edge3.at[g], k, r0, 2)
            ypp = jnp.where(lane_c >= cols - 2, side, pltpu.roll(mid, cols - 2, 1))
            ymm = jnp.where(lane_c < 2, side, pltpu.roll(mid, 2, 1))
            yp = jnp.where(lane_c == cols - 1, near, pltpu.roll(mid, cols - 1, 1))
            ym = jnp.where(lane_c == 0, near, pltpu.roll(mid, 1, 1))
            half = 0.5 / (2.0 + 0.5 * (jnp.abs(xp - xm) + jnp.abs(yp - ym)))
            c = [half * (1.0 + jnp.maximum(far - mid, 0.0)) for far in (xpp, xmm, ypp, ymm)]
            for ref, v in zip((cxp, cxm, cyp, cym), c):
                ref[k, r0:r0 + CHUNK, :] = v
            flow(d0, d1, base, c, None, g, k, r0)
        edge_rows(xs.at[base * GROUPS + g], d1, k, 1)
        return carry

    for g in range(GROUPS):
        take_halo(copies[g], SWEEPS, 2, u, g)
        settle()
        take_halo(dens_copies[g], 0, 1, d0, g)
        far = edge2[g]
        lanes2 = lax.broadcasted_iota(jnp.int32, far.shape, 1)
        edge3[g] = jnp.where(
            lax.rem(lanes2, 4) < 2, pltpu.roll(far, cols - 1, 1), pltpu.roll(far, 1, 1)
        )
        each_class(g, functools.partial(weigh, g), 0)
        copies[g] = send_halo(base, 1, g)
        sent.append(copies[g])

    field, into = d1, d0
    for s in range(1, SWEEPS):
        last = s == SWEEPS - 1
        e = None if last else base + s
        for g in range(GROUPS):
            take_halo(copies[g], base + s - 1, 1, field, g)

            def sweep(k, row):
                total = jnp.zeros((8, cols), jnp.float32)
                for r0 in starts:
                    c = [ref[k, r0:r0 + CHUNK, :] for ref in (cxp, cxm, cyp, cym)]
                    total = flow(field, into, e, c, total, g, k, r0)
                if last:
                    return put(row, k, total)
                edge_rows(xs.at[e * GROUPS + g], into, k, 1)
                return row

            rows_of[g] = each_class(g, sweep, zero_row)
            if last:
                send_sums(SWEEPS * GROUPS + g, rows_of[g])
            else:
                copies[g] = send_halo(e, 1, g)
                sent.append(copies[g])
        field, into = into, field

    out_f = pltpu.make_async_copy(field.at[:, pl.ds(PAD, rows), :], fresh_hbm, out_sem.at[1])
    out_f.start()
    means[0:1, :] = sum(
        offset_of(take_sums((SWEEPS - 1) * GROUPS + g, own[g]), lam[g]) for g in range(GROUPS)
    )
    pending += [(SWEEPS, g) for g in range(GROUPS)]
    settle()
    for copies in sent:
        for c in copies:
            c.wait_send()
    total = sum(take_sums(SWEEPS * GROUPS + g, own[g]) for g in range(GROUPS))
    means[1:2, :] = total * (1.0 / cells)
    for s in range((SWEEPS + 1) * GROUPS):
        pltpu.make_async_copy(arx_in.at[s], arx_in.at[s], axs_sem.at[s]).wait()
        pltpu.make_async_copy(ary_in.at[s], ary_in.at[s], ays_sem.at[s]).wait()
    out_t.wait()
    out_f.wait()


def shards(cost, density_start, coupling):
    nx, ny = lax.axis_size("gx"), lax.axis_size("gy")
    classes, rows, cols = cost.shape
    f32 = jnp.float32
    full = pltpu.VMEM((classes, rows, cols), f32)
    padded = pltpu.VMEM((classes, rows + 2 * PAD, cols), f32)
    slots = 2 * SWEEPS * GROUPS
    some = classes // GROUPS
    sums = (SWEEPS + 1) * GROUPS
    block = rows * 2 * some // cols
    trial, fresh, means = pl.pallas_call(
        functools.partial(kernel, nx, ny),
        out_shape=(
            jax.ShapeDtypeStruct(cost.shape, f32),
            jax.ShapeDtypeStruct(cost.shape, f32),
            jax.ShapeDtypeStruct((2, cols), f32),
        ),
        in_specs=[
            pl.BlockSpec(memory_space=pl.ANY),
            pl.BlockSpec(memory_space=pl.ANY),
            pl.BlockSpec(memory_space=pltpu.SMEM),
        ],
        out_specs=(
            pl.BlockSpec(memory_space=pl.ANY),
            pl.BlockSpec(memory_space=pl.ANY),
            pl.BlockSpec(memory_space=pltpu.VMEM),
        ),
        scratch_shapes=[
            full, padded, full, full, padded, padded, full, full, full, full,
            pltpu.VMEM((slots, 2, 1, some, cols), f32),
            pltpu.VMEM((slots, 2, 1, some, cols), f32),
            pltpu.VMEM((slots, block, cols), f32),
            pltpu.VMEM((slots, 2, block, cols), f32),
            pltpu.VMEM((GROUPS, 2, 2, some, cols), f32),
            pltpu.VMEM((GROUPS, 2, 2, some, cols), f32),
            pltpu.VMEM((GROUPS, 2 * block, cols), f32),
            pltpu.VMEM((GROUPS, 2, 2 * block, cols), f32),
            pltpu.VMEM((GROUPS, block, cols), f32),
            pltpu.VMEM((GROUPS, 2 * block, cols), f32),
            pltpu.VMEM((GROUPS, 2 * block, cols), f32),
            pltpu.VMEM((sums, 1, cols), f32),
            pltpu.VMEM((sums, nx - 1, 1, cols), f32),
            pltpu.VMEM((sums, 1, cols), f32),
            pltpu.VMEM((sums, ny - 1, 1, cols), f32),
            pltpu.VMEM((classes, 1, cols), f32),
            pltpu.SemaphoreType.DMA((2,)),
            pltpu.SemaphoreType.DMA((2,)),
            pltpu.SemaphoreType.DMA((slots, 4)),
            pltpu.SemaphoreType.DMA((slots, 4)),
            pltpu.SemaphoreType.DMA((sums,)),
            pltpu.SemaphoreType.DMA((sums,)),
            pltpu.SemaphoreType.DMA((sums,)),
            pltpu.SemaphoreType.DMA((sums,)),
        ],
        compiler_params=pltpu.CompilerParams(
            collective_id=0, has_side_effects=True, vmem_limit_bytes=67043328
        ),
    )(cost, density_start, coupling)
    offset = means[0, :classes]
    mass = means[1, :classes]
    value = trial - offset[:, None, None]
    density = fresh / mass[:, None, None]
    return value, density, THETA * offset


def solution(mesh):
    placed = P(None, "gx", "gy")
    return jax.shard_map(
        shards,
        mesh=mesh,
        in_specs=(placed, placed, P()),
        out_specs=(placed, placed, P()),
        check_vma=False,
    )
```

time: 85.2 us -> 87.9 us (1.032)
  Pallas kernels: 80.1 us -> 82.8 us
    pallas_call x1, Pallas kernels: 80.1 us -> 82.8 us  [shards(): pl.pallas_call(functools.partial(kernel, nx, ny), out_shape=(jax.ShapeDty...]
where the time goes in v3:
time: 87.9 us; the launch traced here: 87.6 us
  Pallas kernels  82.8 us (94%)
  other arithmetic  3.53 us (4%)
    pallas_call x1, Pallas kernels, shards(): pl.pallas_call(functools.partial(kernel, nx, ny), out_shape=(jax.ShapeDty...  82.8 us
    div x1, other arithmetic, shards(): density = fresh / mass[:, None, None]  3.02 us

profile of v3, /device:TPU:0, one launch (start us, length us, event | category | flops | bytes accessed | tf_op | source)
XLA Modules:
  0.0 87.6 jit_solution(10609054653683999012)
XLA Ops:
  0.6 82.8 %shard_map.58 = (f32[16,128,128]{2,1,0:T(8,128)}, f32[16,128,128]{2,1,0:T(8,128)}, f32[2,128]{1,0:T(2,128)}) custom-call(f32[16,128,128]{2,1,0:T(8,128)} %cost_hbm.1, f32[16,128,128]{2,1,0:T(8,128)} %dens_hbm.1, f32[16,16]{1,0:T(8,128)} %coupling.1), custom_call_target="tpu_custom_call" | custom-call | tf_op jit(solution)/shard_map/pallas_call | solution.py:365
  83.4 0.0 copy-start
  83.4 0.6 copy-done
  84.1 0.5 broadcast_multiply_fusion
  84.6 3.0 %broadcast_divide_fusion = (f32[16,128,128]{2,1,0:T(8,128)}, f32[16,128,128]{2,1,0:T(8,128)}) fusion(f32[16,128,128]{2,1,0:T(8,128)} %get-tuple-element.8, f32[16]{0:T(128)S(1)} %get-tuple-element.9, f32[16,128,128]{2,1,0:T(8,128)} %get-tuple-element.6, f32[16]{0:T(128)S(1)} %get-tuple-element.10), kind=kLoop, calls=%fused_computation | loop fusion | flops 524288 | bytes 4194432 | tf_op jit(solution)/shard_map/div | solution.py:416
  (1 shorter events, 0.0 us)
Async XLA Ops:
  83.4 0.7 copy-start
